TPU v7x, 32 devices: a whole 2x2x4 slice. The times are simulated.
32 devices in a mesh: dp: 1, tp: 32 (over x, y, z, core).
Axes of the slice: x: 2, y: 2, z: 4, core: 2. Of those that a mesh axis runs over, the one named last changes fastest.
Arguments:
- x: bfloat16 [2048, 8192], P('dp')
- dy: bfloat16 [2048, 8192], P('dp')
- gate: bfloat16 [2048, 32768], P('dp', 'tp')
- up: bfloat16 [2048, 32768], P('dp', 'tp')
- w_gate: bfloat16 [8192, 32768], P(None, 'tp')
- w_up: bfloat16 [8192, 32768], P(None, 'tp')
- w_down: bfloat16 [32768, 8192], P('tp')
Outputs:
- output 1: bfloat16 [2048, 8192], P('dp')
- output 2: bfloat16 [8192, 32768], P('dp', 'tp')
- output 3: bfloat16 [8192, 32768], P('dp', 'tp')
- output 4: bfloat16 [32768, 8192], P(('dp', 'tp'))
All inputs are finite; a program needn't handle non-finite values.
Results may differ from a plain program's by a relative error of at most 0.012.
Values are sent between devices in bfloat16 or wider.
A program may use at most 2 GiB of HBM per device.

v0:
```python
import jax
import jax.numpy as jnp
from jax import lax
from jax.sharding import PartitionSpec as P


def act(gate, up):
    return jax.nn.silu(gate) * up


def solution(mesh):
    def step(x, dy, gate, up, w_gate, w_up, w_down):
        hidden, back = jax.vjp(act, gate.astype(jnp.float32), up.astype(jnp.float32))
        d_hidden = jnp.dot(dy, w_down.T, preferred_element_type=jnp.float32)
        d_gate, d_up = (g.astype(jnp.bfloat16) for g in back(d_hidden))
        term = jnp.dot(d_gate, w_gate.T, preferred_element_type=jnp.float32) + jnp.dot(d_up, w_up.T, preferred_element_type=jnp.float32)
        dx = lax.psum(term.astype(jnp.bfloat16), "tp")
        dw_gate = jnp.dot(x.T, d_gate, preferred_element_type=jnp.float32)
        dw_up = jnp.dot(x.T, d_up, preferred_element_type=jnp.float32)
        dw_down = jnp.dot(hidden.astype(jnp.bfloat16).T, dy, preferred_element_type=jnp.float32)
        return dx, *(g.astype(jnp.bfloat16) for g in (dw_gate, dw_up, dw_down))

    tokens, columns, rows = P("dp", None), P(None, "tp"), P("tp", None)
    return jax.shard_map(
        step,
        mesh=mesh,
        in_specs=(tokens, tokens, P("dp", "tp"), P("dp", "tp"), columns, columns, rows),
        out_specs=(tokens, P("dp", "tp"), P("dp", "tp"), P(("dp", "tp"), None)),
        check_vma=False,
    )
```

profile of v0, /device:TPU:0, one launch (start us, length us, event | category | flops | bytes accessed | tf_op | source)
XLA Modules:
  0.0 699.5 jit_solution(7892661001765965485)
XLA Ops:
  7.2 0.0 all-reduce.2.cloned.1.call-start
  7.2 65.0 %fusion.6 = (bf16[2048,1024]{1,0:T(8,128)(2,1)}, f32[2048,1024]{1,0:T(8,128)}) fusion(bf16[2048,1024]{1,0:T(8,128)(2,1)} %param.9, bf16[2048,1024]{1,0:T(8,128)(2,1)} %param.10, bf16[2048,8192]{1,0:T(8,128)(2,1)} %param.8, bf16[1024,8192]{1,0:T(8,128)(2,1)} %param.13), kind=kOutput, calls=%fused_computation.16 | convolution fusion | flops 34387001344 | bytes 71303168 | tf_op jit(solution)/shard_map/dot_general | solution.py:14
  72.2 45.4 %fusion.9 = f32[2048,8192]{1,0:T(8,128)} fusion(bf16[2048,1024]{1,0:T(8,128)(2,1)} %get-tuple-element.8, bf16[8192,1024]{1,0:T(8,128)(2,1)} %param.11), kind=kOutput, calls=%fused_computation.19 | convolution fusion | flops 34359738368 | bytes 88080384 | tf_op jit(solution)/shard_map/dot_general | solution.py:16
  117.6 53.3 %add_convert_fusion = bf16[2048,8192]{1,0:T(8,128)(2,1)} fusion(f32[2048,8192]{1,0:T(8,128)} %fusion.9, bf16[8192,1024]{1,0:T(8,128)(2,1)} %param.12, f32[2048,1024]{1,0:T(8,128)} %get-tuple-element.9, bf16[2048,1024]{1,0:T(8,128)(2,1)} %param.9), kind=kOutput, calls=%fused_computation | convolution fusion | flops 34407972864 | bytes 130023424 | tf_op jit(solution)/shard_map/dot_general | solution.py:16
  170.9 0.0 all-reduce.2.cloned.1.call-update
  170.9 42.8 %convert_bitcast_fusion.1 = bf16[8192,1024]{0,1:T(8,128)(2,1)} fusion(bf16[2048,1024]{1,0:T(8,128)(2,1)} %get-tuple-element.8, bf16[2048,8192]{1,0:T(8,128)(2,1)} %param.7), kind=kOutput, calls=%fused_computation.2 | convolution fusion | flops 34368126976 | bytes 54525952 | tf_op jit(solution)/shard_map/dot_general | solution.py:18
  213.8 22.4 %copy.11 = bf16[8192,1024]{1,0:T(8,128)(2,1)} copy(bf16[8192,1024]{0,1:T(8,128)(2,1)} %convert_bitcast_fusion.1) | data formatting | bytes 33554432
  236.1 47.7 %convert_bitcast_fusion = bf16[8192,1024]{0,1:T(8,128)(2,1)} fusion(bf16[2048,8192]{1,0:T(8,128)(2,1)} %param.7, f32[2048,1024]{1,0:T(8,128)} %get-tuple-element.9, bf16[2048,1024]{1,0:T(8,128)(2,1)} %param.9), kind=kOutput, calls=%fused_computation.1 | convolution fusion | flops 34382807040 | bytes 62914560 | tf_op jit(solution)/shard_map/dot_general | solution.py:19
  283.8 22.4 %copy.12 = bf16[8192,1024]{1,0:T(8,128)(2,1)} copy(bf16[8192,1024]{0,1:T(8,128)(2,1)} %convert_bitcast_fusion) | data formatting | bytes 33554432
  306.2 49.7 %convolution_convert_fusion = bf16[1024,8192]{1,0:T(8,128)(2,1)} fusion(bf16[2048,8192]{1,0:T(8,128)(2,1)} %param.8, bf16[2048,1024]{1,0:T(8,128)(2,1)} %param.10, bf16[2048,1024]{1,0:T(8,128)(2,1)} %param.9), kind=kOutput, calls=%fused_computation.3 | convolution fusion | flops 34384904192 | bytes 58720256 | tf_op jit(solution)/shard_map/dot_general | solution.py:20
  355.9 313.4 %all-reduce.2.cloned.1.call-done = bf16[2048,8192]{1,0:T(8,128)(2,1)} async-done(((bf16[2048,8192]{1,0:T(8,128)(2,1)}), bf16[2048,8192]{1,0:T(8,128)(2,1)}) %all-reduce.2.cloned.1.call-update) | async-done | bytes 33554448 | tf_op jit(solution)/shard_map/psum | solution.py:17
  669.2 23.0 %copy.14 = bf16[2048,8192]{1,0:T(8,128)(2,1)} copy(bf16[2048,8192]{1,0:T(8,128)(2,1)} %all-reduce.2.cloned.1.call-done) | data formatting | bytes 67108864
Async XLA Ops:
  7.2 662.1 %all-reduce.2.cloned.1.call-start = ((), (), s32[]{:S(2)}) async-start(), calls=%async_computation | async-start | bytes 67108864 | tf_op jit(solution)/shard_map/psum | solution.py:17
Sparse Core Ops, SparseCore 0:
  171.1 498.1 all-reduce.1
where the time goes:
time: 704 us; the launch traced here: 700 us
  waiting for transfers between devices  313 us (44%)
  matrix products  304 us (43%)
  local copies, waits for them, and re-layouts  67.8 us (10%)
  between operations  14.5 us (2%)
    psum x1, waiting for transfers between devices, step(): dx = lax.psum(term.astype(jnp.bfloat16), 'tp')  313 us
    unnamed x3, local copies, waits for them, and re-layouts  67.8 us
    dot_general x1, matrix products, step(): d_hidden = jnp.dot(dy, w_down.T, preferred_element_type=jnp.float32)  65 us
    dot_general x1, matrix products, step(): jnp.dot(d_up, w_up.T, preferred_element_type=jnp.float32)  53.3 us
    dot_general x1, matrix products, step(): jnp.dot(hidden.astype(jnp.bfloat16).T, dy, preferred_element_type=jnp.flo...  49.7 us
    dot_general x1, matrix products, step(): dw_up = jnp.dot(x.T, d_up, preferred_element_type=jnp.float32)  47.7 us
    dot_general x1, matrix products, step(): jnp.dot(d_gate, w_gate.T, preferred_element_type=jnp.float32)  45.4 us
    dot_general x1, matrix products, step(): dw_gate = jnp.dot(x.T, d_gate, preferred_element_type=jnp.float32)  42.8 us
  transfers between devices with their start and end apart: 1, of which 1 were waited for; matrix products, arithmetic and copies ran while one was open for 26% of the time, Pallas kernels for 0%

commit v1 on v0

v1 whole, which is shorter than its diff:
```python
import functools

import jax
import jax.numpy as jnp
from jax import lax
from jax.experimental import pallas as pl
from jax.experimental.pallas import tpu as pltpu
from jax.sharding import PartitionSpec as P

BF, F32 = jnp.bfloat16, jnp.float32
MESH = pl.DeviceIdType.MESH
NT = (((1,), (1,)), ((), ()))
TN = (((0,), (0,)), ((), ()))

QUARTERS = 4
COLS = 8
CHUNKS = QUARTERS * COLS
KBLOCKS = 4
UNITS = 16
DH = QUARTERS * KBLOCKS
E1, E2, E3, E4, E5, E6, E7, E8, E9, E10, E11, E12 = 1, 5, 8, 10, 12, 14, 15, 17, 19, 22, 26, 28
FIRST = KBLOCKS
DW_GROUP = (DH - KBLOCKS) // 2
TICKS = FIRST + max(4 * (DW_GROUP + UNITS), 2 * CHUNKS + E12)


def dot(a, b, dims):
    return lax.dot_general(a, b, dims, preferred_element_type=F32)


def add_rows(dst, a, b, rows, block):
    def body(i, _):
        r = pl.ds(pl.multiple_of(i * block, block), block)
        dst[r] = (a[r].astype(F32) + b[r].astype(F32)).astype(BF)

    lax.fori_loop(0, rows // block, body, None)


def main_kernel(
    x, dy, gate, up, w_gate, w_up, w_down, dx, hid, dw,
    d, w_buf, wd_buf, dy_buf, x_buf, g_buf, u_buf, acc, h_buf, o_buf,
    term, r_d, s1, r_1, s2, z_r, z_l, r_3,
    w_sem, dh_sem, x_sem, gu_sem, h_sem, o_sem, loc_sem,
    d_snd, d_rcv, s1_snd, s1_rcv, zr_snd, zr_rcv, zl_snd, zl_rcv, s3_snd, s3_rcv,
    a3_snd, a3_rcv, gr_snd, gr_rcv, gl_snd, gl_rcv, a1_snd, a1_rcv, ad_snd, ad_rcv,
):
    rows, cols = dy.shape
    ff = gate.shape[1]
    qr, nc, kb, xt = rows // QUARTERS, cols // COLS, cols // KBLOCKS, cols // UNITS
    half, quart, piece, last = qr // 2, qr // 4, qr // 16, qr // 32

    me = lax.axis_index("tp")
    core, z = lax.rem(me, 2), lax.rem(lax.div(me, 2), 4)
    y, xx = lax.rem(lax.div(me, 8), 2), lax.div(me, 16)
    n_d = me + 1 - 2 * core
    n_x, n_y = me + 16 * (1 - 2 * xx), me + 8 * (1 - 2 * y)
    n_r, n_l = me + 2, me - 2

    def copy(src, dst, sem):
        return pltpu.make_async_copy(src, dst, sem)

    def remote(src, dst, snd, rcv, to):
        return pltpu.make_async_remote_copy(
            src_ref=src, dst_ref=dst, send_sem=snd, recv_sem=rcv,
            device_id={"tp": to}, device_id_type=MESH,
        )

    def dh_loads(m):
        q, j, slot = lax.div(m, KBLOCKS), lax.rem(m, KBLOCKS), lax.rem(m, 2)
        k = pl.ds(pl.multiple_of(j * kb, kb), kb)
        r = pl.ds(pl.multiple_of(q * qr, qr), qr)
        return (
            copy(dy.at[r, k], dy_buf.at[slot], dh_sem.at[0, slot]),
            copy(w_down.at[:, k], wd_buf.at[slot], dh_sem.at[1, slot]),
        )

    def gu_loads(q):
        r = pl.ds(pl.multiple_of(q * qr, qr), qr)
        return copy(gate.at[r], g_buf, gu_sem.at[0]), copy(up.at[r], u_buf, gu_sem.at[1])

    def w_loads(k):
        slot = lax.rem(k, 2)
        r = pl.ds(pl.multiple_of(lax.rem(k, COLS) * nc, nc), nc)
        return (
            copy(w_gate.at[r], w_buf.at[slot, :, pl.ds(0, ff)], w_sem.at[0, slot]),
            copy(w_up.at[r], w_buf.at[slot, :, pl.ds(ff, ff)], w_sem.at[1, slot]),
        )

    def x_load(u):
        slot = lax.rem(u, 2)
        return copy(x.at[:, pl.ds(pl.multiple_of(u * xt, xt), xt)], x_buf.at[slot], x_sem.at[slot])

    def o_store(u, j):
        return copy(o_buf.at[j], dw.at[j, pl.ds(pl.multiple_of(u * xt, xt), xt)], o_sem.at[j])

    def h_store(q):
        return copy(h_buf, hid.at[pl.ds(pl.multiple_of(q * qr, qr), qr)], h_sem)

    def go(*copies):
        for c in copies:
            c.start()

    def wait(*copies):
        for c in copies:
            c.wait()

    go(*dh_loads(0))
    go(*dh_loads(1))
    go(*gu_loads(0))
    go(*w_loads(0))
    go(*w_loads(1))

    barrier = pltpu.get_barrier_semaphore()
    for to in (n_d, n_x, n_y):
        pl.semaphore_signal(barrier, inc=1, device_id={"tp": to}, device_id_type=MESH)

    @pl.when(z > 0)
    def _():
        pl.semaphore_signal(barrier, inc=1, device_id={"tp": n_l}, device_id_type=MESH)

    @pl.when(z < 3)
    def _():
        pl.semaphore_signal(barrier, inc=1, device_id={"tp": n_r}, device_id_type=MESH)

    pl.semaphore_wait(barrier, jnp.where((z > 0) & (z < 3), 5, 4))

    def chunk(k):
        q, n, odd = lax.div(k, COLS), lax.rem(k, COLS), lax.rem(k, 2)
        b1, b3 = jnp.where(odd == 0, xx, y), jnp.where(odd == 0, y, xx)
        to1, to3 = jnp.where(odd == 0, n_x, n_y), jnp.where(odd == 0, n_y, n_x)
        return q * qr, n * nc, b1, b3, to1, to3

    def at_out(row, count, col):
        return dx.at[pl.ds(pl.multiple_of(row, last), count), pl.ds(pl.multiple_of(col, nc), nc)]

    def send_d(k):
        s = lax.rem(k, 2)
        src = term.at[s, pl.ds(pl.multiple_of((1 - core) * half, half), half)]
        return remote(src, r_d.at[lax.rem(k, 4)], d_snd.at[s], d_rcv.at[lax.rem(k, 4)], n_d)

    def send_1(k):
        _, _, b1, _, to1, _ = chunk(k)
        src = s1.at[lax.rem(k, 4), pl.ds(pl.multiple_of((1 - b1) * quart, quart), quart)]
        return remote(src, r_1.at[lax.rem(k, 8)], s1_snd.at[lax.rem(k, 4)], s1_rcv.at[lax.rem(k, 8)], to1)

    def send_zr(k, row, count):
        s = lax.rem(k, 8)
        return remote(s2.at[s, pl.ds(row, count)], z_r.at[s, pl.ds(0, count)], zr_snd.at[s], zr_rcv.at[s], n_r)

    def send_zl(k, row, count):
        s = lax.rem(k, 8)
        return remote(s2.at[s, pl.ds(row, count)], z_l.at[s, pl.ds(0, count)], zl_snd.at[s], zl_rcv.at[s], n_l)

    def send_3(k):
        _, _, _, b3, _, to3 = chunk(k)
        src = s2.at[lax.rem(k, 8), pl.ds(pl.multiple_of(z * piece + (1 - b3) * last, last), last)]
        return remote(src, r_3.at[lax.rem(k, 4)], s3_snd.at[lax.rem(k, 4)], s3_rcv.at[lax.rem(k, 4)], to3)

    def final_rows(k):
        row, col, b1, b3, _, _ = chunk(k)
        return (
            s2.at[lax.rem(k, 8), pl.ds(pl.multiple_of(z * piece + b3 * last, last), last)],
            at_out(row + core * half + b1 * quart + z * piece + b3 * last, last, col),
        )

    def keep_final(k):
        src, dst = final_rows(k)
        return copy(src, dst, loc_sem.at[lax.rem(k, 4)])

    def gather_3(k):
        src, dst = final_rows(k)
        s = lax.rem(k, 8)
        return remote(src, dst, a3_snd.at[s], a3_rcv.at[s], chunk(k)[5])

    def gather_r(k, first, count):
        row, col, b1, _, _, _ = chunk(k)
        ref = at_out(row + core * half + b1 * quart + first * piece, count * piece, col)
        s = lax.rem(k, 8)
        return remote(ref, ref, gr_snd.at[s], gr_rcv.at[s], n_r)

    def gather_l(k, first, count):
        row, col, b1, _, _, _ = chunk(k)
        ref = at_out(row + core * half + b1 * quart + first * piece, count * piece, col)
        s = lax.rem(k, 8)
        return remote(ref, ref, gl_snd.at[s], gl_rcv.at[s], n_l)

    def gather_1(k):
        row, col, b1, _, to1, _ = chunk(k)
        ref = at_out(row + core * half + b1 * quart, quart, col)
        s = lax.rem(k, 8)
        return remote(ref, ref, a1_snd.at[s], a1_rcv.at[s], to1)

    def gather_d(k):
        row, col, _, _, _, _ = chunk(k)
        ref = at_out(row + core * half, half, col)
        s = lax.rem(k, 8)
        return remote(ref, ref, ad_snd.at[s], ad_rcv.at[s], n_d)

    blk = piece

    def e12(k):
        gather_d(k).wait_recv()
        gather_1(k).wait_send()
        gather_d(k).wait_send()
        for zz, right, left in ((0, (0, 1), None), (1, (0, 2), (1, 3)), (2, (0, 3), (2, 2)), (3, None, (3, 1))):

            @pl.when(z == zz)
            def _(right=right, left=left):
                if right:
                    gather_r(k, *right).wait_send()
                if left:
                    gather_l(k, *left).wait_send()

    def e11(k):
        gather_1(k).wait_recv()
        gather_d(k).start()

    def e10(k):
        @pl.when(z == 3)
        def _():
            gather_r(k, 0, 3).wait_recv()

        @pl.when(z == 0)
        def _():
            gather_l(k, 1, 3).wait_recv()

        gather_1(k).start()

    def e9(k):
        @pl.when(z == 2)
        def _():
            gather_r(k, 0, 2).wait_recv()
            gather_r(k, 0, 3).start()

        @pl.when(z == 1)
        def _():
            gather_l(k, 2, 2).wait_recv()
            gather_l(k, 1, 3).start()

    def e8(k):
        gather_3(k).wait_send()

        @pl.when(z == 1)
        def _():
            gather_r(k, 0, 1).wait_recv()
            gather_r(k, 0, 2).start()

        @pl.when(z == 2)
        def _():
            gather_l(k, 3, 1).wait_recv()
            gather_l(k, 2, 2).start()

    def e7(k):
        keep_final(k).wait()
        gather_3(k).wait_recv()

        @pl.when(z == 0)
        def _():
            gather_r(k, 0, 1).start()

        @pl.when(z == 3)
        def _():
            gather_l(k, 3, 1).start()

    def e6(k):
        s = lax.rem(k, 8)
        _, _, _, b3, _, _ = chunk(k)
        send_3(k).wait()
        mine = s2.at[s, pl.ds(pl.multiple_of(z * piece + b3 * last, last), last)]
        add_rows(mine, mine, r_3.at[lax.rem(k, 4)], last, last)
        for zz, right, left in (
            (0, (1, 3), None), (1, (2, 2), (0, 1)), (2, (3, 1), (0, 2)), (3, None, (0, 3)),
        ):

            @pl.when(z == zz)
            def _(right=right, left=left):
                if right:
                    send_zr(k, right[0] * piece, right[1] * piece).wait_send()
                if left:
                    send_zl(k, left[0] * piece, left[1] * piece).wait_send()

        keep_final(k).start()
        gather_3(k).start()

    def add_piece(k, buf, first, count):
        s = lax.rem(k, 8)
        mine = s2.at[s, pl.ds(first * piece, count * piece)]
        add_rows(mine, mine, buf.at[s, pl.ds(0, count * piece)], count * piece, blk)

    def e5(k):
        @pl.when(z == 3)
        def _():
            send_zr(k, 3 * piece, piece).wait_recv()
            add_piece(k, z_r, 3, 1)

        @pl.when(z == 0)
        def _():
            send_zl(k, 0, piece).wait_recv()
            add_piece(k, z_l, 0, 1)

        send_3(k).start()

    def e4(k):
        @pl.when(z == 2)
        def _():
            send_zr(k, 2 * piece, 2 * piece).wait_recv()
            add_piece(k, z_r, 2, 2)
            send_zr(k, 3 * piece, piece).start()

        @pl.when(z == 1)
        def _():
            send_zl(k, 0, 2 * piece).wait_recv()
            add_piece(k, z_l, 0, 2)
            send_zl(k, 0, piece).start()

    def e3(k):
        @pl.when(z == 1)
        def _():
            send_zr(k, piece, 3 * piece).wait_recv()
            add_piece(k, z_r, 1, 3)
            send_zr(k, 2 * piece, 2 * piece).start()

        @pl.when(z == 2)
        def _():
            send_zl(k, 0, 3 * piece).wait_recv()
            add_piece(k, z_l, 0, 3)
            send_zl(k, 0, 2 * piece).start()

    def e2(k):
        _, _, b1, _, _, _ = chunk(k)
        send_1(k).wait()
        kept = s1.at[lax.rem(k, 4), pl.ds(pl.multiple_of(b1 * quart, quart), quart)]
        add_rows(s2.at[lax.rem(k, 8)], kept, r_1.at[lax.rem(k, 8)], quart, blk)

        @pl.when(z == 0)
        def _():
            send_zr(k, piece, 3 * piece).start()

        @pl.when(z == 3)
        def _():
            send_zl(k, 0, 3 * piece).start()

    def e1(k):
        _, _, b1, _, _, _ = chunk(k)
        send_d(k).wait_recv()
        for b in (1 - b1, b1):
            r = pl.ds(pl.multiple_of(b * quart, quart), quart)
            own = pl.ds(pl.multiple_of(core * half + b * quart, quart), quart)
            add_rows(
                s1.at[lax.rem(k, 4), r], term.at[lax.rem(k, 2), own], r_d.at[lax.rem(k, 4), r], quart, blk
            )
        send_d(k).wait_send()
        send_1(k).start()

    def activation(q):
        wait(*gu_loads(q))

        @pl.when(q > 0)
        def _():
            h_store(q - 1).wait()

        step = min(16, qr)

        def body(i, _):
            r = pl.ds(pl.multiple_of(i * step, step), step)
            to = pl.ds(pl.multiple_of(q * qr + i * step, step), step)
            g, u, dh = g_buf[r].astype(F32), u_buf[r].astype(F32), acc[r]
            sig = jax.nn.sigmoid(g)
            silu = g * sig
            h_buf[r] = (silu * u).astype(BF)
            d[to, pl.ds(ff, ff)] = (dh * silu).astype(BF)
            d[to, pl.ds(0, ff)] = (dh * u * (sig + silu * (1.0 - sig))).astype(BF)

        lax.fori_loop(0, qr // step, body, None)
        h_store(q).start()

        @pl.when(q + 1 < QUARTERS)
        def _():
            go(*gu_loads(q + 1))

    def dh_tile(m):
        q, j, slot = lax.div(m, KBLOCKS), lax.rem(m, KBLOCKS), lax.rem(m, 2)
        wait(*dh_loads(m))
        acc[...] = jnp.where(j == 0, 0.0, acc[...]) + dot(dy_buf[slot], wd_buf[slot], NT)

        @pl.when(m + 2 < DH)
        def _():
            go(*dh_loads(m + 2))

        @pl.when(j == KBLOCKS - 1)
        def _():
            activation(q)

    def dx_tile(k):
        slot = lax.rem(k, 2)
        r = pl.ds(pl.multiple_of(lax.div(k, COLS) * qr, qr), qr)
        wait(*w_loads(k))
        term[slot] = dot(d[r], w_buf[slot], NT).astype(BF)

        @pl.when(k + 2 < CHUNKS)
        def _():
            go(*w_loads(k + 2))

    def dw_tile(u, j):
        slot = lax.rem(u, 2)

        @pl.when(j == 0)
        def _():
            x_load(u).wait()

        @pl.when(u > 0)
        def _():
            o_store(u - 1, j).wait()

        o_buf[j] = dot(x_buf[slot], d[:, pl.ds(pl.multiple_of(j * ff, ff), ff)], TN).astype(BF)
        o_store(u, j).start()

        @pl.when((j == 1) & (u + 2 < UNITS))
        def _():
            x_load(u + 2).start()

    def tick(t, _):
        g, s = lax.div(t, 4) - 1, lax.rem(t, 4)
        filler = 2 * g + s - 2

        @pl.when((t < FIRST) | ((s >= 2) & (filler < DH - KBLOCKS)))
        def _():
            dh_tile(jnp.where(t < FIRST, t, KBLOCKS + filler))

        @pl.when(t == FIRST)
        def _():
            go(x_load(0), x_load(1))

        @pl.when((t >= FIRST) & (s < 2) & (g < CHUNKS // 2))
        def _():
            dx_tile(2 * g + s)

        @pl.when((s >= 2) & (g >= DW_GROUP) & (g < DW_GROUP + UNITS))
        def _():
            dw_tile(g - DW_GROUP, s - 2)

        for off, event in (
            (E12, e12), (E11, e11), (E10, e10), (E9, e9), (E8, e8), (E7, e7), (E6, e6),
            (E5, e5), (E4, e4), (E3, e3), (E2, e2), (E1, e1), (0, lambda k: send_d(k).start()),
        ):
            at = t - FIRST - off
            k = 2 * lax.div(at, 4) + lax.rem(at, 4)

            @pl.when((at >= 0) & (lax.rem(at, 4) < 2) & (k < CHUNKS))
            def _(event=event, k=k):
                event(k)

    lax.fori_loop(0, TICKS, tick, None)
    h_store(QUARTERS - 1).wait()
    wait(o_store(UNITS - 1, 0), o_store(UNITS - 1, 1))


def main_call(x, dy, gate, up, w_gate, w_up, w_down):
    rows, cols = dy.shape
    ff = gate.shape[1]
    qr, nc, kb, xt = rows // QUARTERS, cols // COLS, cols // KBLOCKS, cols // UNITS
    half, quart, piece, last = qr // 2, qr // 4, qr // 16, qr // 32
    dma = pltpu.SemaphoreType.DMA
    vmem = pltpu.VMEM
    anywhere = pl.BlockSpec(memory_space=pl.ANY)
    flops = 2 * rows * cols * ff * 5
    return pl.pallas_call(
        main_kernel,
        out_shape=(
            jax.ShapeDtypeStruct((rows, cols), BF),
            jax.ShapeDtypeStruct((rows, ff), BF),
            jax.ShapeDtypeStruct((2, cols, ff), BF),
        ),
        in_specs=[anywhere] * 7,
        out_specs=(anywhere,) * 3,
        scratch_shapes=[
            vmem((rows, 2 * ff), BF),
            vmem((2, nc, 2 * ff), BF),
            vmem((2, ff, kb), BF),
            vmem((2, qr, kb), BF),
            vmem((2, rows, xt), BF),
            vmem((qr, ff), BF),
            vmem((qr, ff), BF),
            vmem((qr, ff), F32),
            vmem((qr, ff), BF),
            vmem((2, xt, ff), BF),
            vmem((2, qr, nc), BF),
            vmem((4, half, nc), BF),
            vmem((4, half, nc), BF),
            vmem((8, quart, nc), BF),
            vmem((8, quart, nc), BF),
            vmem((8, 3 * piece, nc), BF),
            vmem((8, 3 * piece, nc), BF),
            vmem((4, last, nc), BF),
            dma((2, 2)), dma((2, 2)), dma((2,)), dma((2,)), dma, dma((2,)), dma((4,)),
            dma((2,)), dma((4,)), dma((4,)), dma((8,)),
            dma((8,)), dma((8,)), dma((8,)), dma((8,)), dma((4,)), dma((4,)),
            dma((8,)), dma((8,)), dma((8,)), dma((8,)), dma((8,)), dma((8,)),
            dma((8,)), dma((8,)), dma((8,)), dma((8,)),
        ],
        compiler_params=pltpu.CompilerParams(
            collective_id=0, has_side_effects=True, vmem_limit_bytes=64_000_000
        ),
        cost_estimate=pl.CostEstimate(flops=flops, bytes_accessed=400 << 20, transcendentals=rows * ff),
        name="dx_reduce",
    )(x, dy, gate, up, w_gate, w_up, w_down)


def tail_kernel(hid, dy, dx_in, dw_in, dx, dw_gate, dw_up, dw_down):
    dw_down[...] = dot(hid[...], dy[...], TN).astype(BF)
    dx[...] = dx_in[...]
    dw_gate[...] = dw_in[0]
    dw_up[...] = dw_in[1]


def tail_call(hid, dy, dx, dw):
    rows, cols = dy.shape
    ff = hid.shape[1]
    n = UNITS
    spec = pl.BlockSpec
    return pl.pallas_call(
        tail_kernel,
        grid=(n,),
        out_shape=(
            jax.ShapeDtypeStruct((rows, cols), BF),
            jax.ShapeDtypeStruct((cols, ff), BF),
            jax.ShapeDtypeStruct((cols, ff), BF),
            jax.ShapeDtypeStruct((ff, cols), BF),
        ),
        in_specs=[
            spec((rows, ff), lambda i: (0, 0)),
            spec((rows, cols // n), lambda i: (0, i)),
            spec((rows // n, cols), lambda i: (i, 0)),
            spec((2, cols // n, ff), lambda i: (0, i, 0)),
        ],
        out_specs=(
            spec((rows // n, cols), lambda i: (i, 0)),
            spec((cols // n, ff), lambda i: (i, 0)),
            spec((cols // n, ff), lambda i: (i, 0)),
            spec((ff, cols // n), lambda i: (0, i)),
        ),
        compiler_params=pltpu.CompilerParams(vmem_limit_bytes=60_000_000),
        cost_estimate=pl.CostEstimate(
            flops=2 * rows * cols * ff, bytes_accessed=180 << 20, transcendentals=0
        ),
        name="dw_down_and_copies",
    )(hid, dy, dx, dw)


def solution(mesh):
    def step(x, dy, gate, up, w_gate, w_up, w_down):
        dx, hid, dw = main_call(x, dy, gate, up, w_gate, w_up, w_down)
        return tail_call(hid, dy, dx, dw)

    tokens, columns, rows = P("dp", None), P(None, "tp"), P("tp", None)
    return jax.shard_map(
        step,
        mesh=mesh,
        in_specs=(tokens, tokens, P("dp", "tp"), P("dp", "tp"), columns, columns, rows),
        out_specs=(tokens, P("dp", "tp"), P("dp", "tp"), P(("dp", "tp"), None)),
        check_vma=False,
    )
```

time: 704 us -> 395 us (0.56)
  Pallas kernels: 0 us -> 394 us
  waiting for transfers between devices: 313 us -> 0 us
  matrix products: 304 us -> 0 us
  local copies, waits for them, and re-layouts: 67.8 us -> 0 us
  between operations: 14.5 us -> 0.64 us
    pallas_call x0 -> x2, Pallas kernels: none -> 394 us  [the longest x1 320 us: main_call(): pl.pallas_call(main_kernel, out_shape=(jax.ShapeDtypeStruct((rows, cols),...]
    psum x1 -> x0, waiting for transfers between devices: 313 us -> none  [step(): dx = lax.psum(term.astype(jnp.bfloat16), 'tp')]
    dot_general x6 -> x0, matrix products: 304 us -> none  [the longest x1 65 us: step(): d_hidden = jnp.dot(dy, w_down.T, preferred_element_type=jnp.float32)]
    unnamed x3 -> x0, local copies, waits for them, and re-layouts: 67.8 us -> none
  transfers between devices with their start and end apart: 1 -> 0, of which waited for: 1 -> 0; matrix products, arithmetic and copies ran while one was open for 26% -> 0% of each run, Pallas kernels for 0% -> 0%
where the time goes in v1:
time: 395 us
  Pallas kernels  394 us (100%)
    pallas_call x1, Pallas kernels, main_call(): pl.pallas_call(main_kernel, out_shape=(jax.ShapeDtypeStruct((rows, cols),...  320 us
    pallas_call x1, Pallas kernels, tail_call(): pl.pallas_call(tail_kernel, grid=(n,), out_shape=(jax.ShapeDtypeStruct((r...  74.1 us

profile of v1, /device:TPU:0, one launch (start us, length us, event | category | flops | bytes accessed | tf_op | source)
XLA Modules:
  0.0 395.0 jit_solution(7515620829201035134)
XLA Ops:
  0.6 320.2 %dx_reduce.1 = (bf16[2048,8192]{1,0:T(8,128)(2,1)}, bf16[2048,1024]{1,0:T(8,128)(2,1)}, bf16[2,8192,1024]{2,1,0:T(8,128)(2,1)}) custom-call(bf16[2048,8192]{1,0:T(8,128)(2,1)} %x.1, bf16[2048,8192]{1,0:T(8,128)(2,1)} %dy.3, bf16[2048,1024]{1,0:T(8,128)(2,1)} %gate.1, bf16[2048,1024]{1,0:T(8,128)(2,1)} %up.1, bf16[8192,1024]{1,0:T(8,128)(2,1)} %w_gate.1, ...), custom_call_target="tpu_custom_call" | custom-call | flops 171798691840 | bytes 419430400 | tf_op jit(solution)/shard_map/dx_reduce/pallas_call | solution.py:467
  320.9 74.1 %dw_down_and_copies.1 = (bf16[2048,8192]{1,0:T(8,128)(2,1)}, bf16[8192,1024]{1,0:T(8,128)(2,1)}, bf16[8192,1024]{1,0:T(8,128)(2,1)}, bf16[1024,8192]{1,0:T(8,128)(2,1)}) custom-call(bf16[2048,1024]{1,0:T(8,128)(2,1)} %get-tuple-element.7.hid, bf16[2048,8192]{1,0:T(8,128)(2,1)} %dy.3, bf16[2048,8192]{1,0:T(8,128)(2,1)} %get-tuple-element.8.dx_in, ...), custom_call_target="tpu_custom_call" | custom-call | flops 34359738368 | bytes 188743680 | tf_op jit(solution)/shard_map/dw_down_and_copies/pallas_call | solution.py:521

commit v2 on v1

--- a/solution.py
+++ b/solution.py
@@ -1,5 +1,3 @@
-import functools
-
 import jax
 import jax.numpy as jnp
 from jax import lax
@@ -18,10 +16,10 @@
 KBLOCKS = 4
 UNITS = 16
 DH = QUARTERS * KBLOCKS
-E1, E2, E3, E4, E5, E6, E7, E8, E9, E10, E11, E12 = 1, 5, 8, 10, 12, 14, 15, 17, 19, 22, 26, 28
+E1, E2, E3, E4, E5, E6, E7, E8, E9, E10, E11, E12 = 1, 4, 7, 9, 11, 12, 14, 16, 18, 23, 33, 38
 FIRST = KBLOCKS
-DW_GROUP = (DH - KBLOCKS) // 2
-TICKS = FIRST + max(4 * (DW_GROUP + UNITS), 2 * CHUNKS + E12)
+FILLERS = DH - KBLOCKS + 2 * UNITS
+TICKS = FIRST + max(2 * FILLERS, 2 * CHUNKS + E12)
 
 
 def dot(a, b, dims):
@@ -187,13 +185,13 @@
     def gather_1(k):
         row, col, b1, _, to1, _ = chunk(k)
         ref = at_out(row + core * half + b1 * quart, quart, col)
-        s = lax.rem(k, 8)
+        s = lax.rem(k, 16)
         return remote(ref, ref, a1_snd.at[s], a1_rcv.at[s], to1)
 
     def gather_d(k):
         row, col, _, _, _, _ = chunk(k)
         ref = at_out(row + core * half, half, col)
-        s = lax.rem(k, 8)
+        s = lax.rem(k, 16)
         return remote(ref, ref, ad_snd.at[s], ad_rcv.at[s], n_d)
 
     blk = piece
@@ -420,33 +418,34 @@
             x_load(u + 2).start()
 
     def tick(t, _):
-        g, s = lax.div(t, 4) - 1, lax.rem(t, 4)
-        filler = 2 * g + s - 2
-
-        @pl.when((t < FIRST) | ((s >= 2) & (filler < DH - KBLOCKS)))
-        def _():
-            dh_tile(jnp.where(t < FIRST, t, KBLOCKS + filler))
+        i, s = lax.div(t - FIRST, 2), lax.rem(t, 2)
+
+        @pl.when((t < FIRST) | ((s == 1) & (i < DH - KBLOCKS)))
+        def _():
+            dh_tile(jnp.where(t < FIRST, t, KBLOCKS + i))
 
         @pl.when(t == FIRST)
         def _():
             go(x_load(0), x_load(1))
 
-        @pl.when((t >= FIRST) & (s < 2) & (g < CHUNKS // 2))
-        def _():
-            dx_tile(2 * g + s)
-
-        @pl.when((s >= 2) & (g >= DW_GROUP) & (g < DW_GROUP + UNITS))
-        def _():
-            dw_tile(g - DW_GROUP, s - 2)
+        @pl.when((t >= FIRST) & (s == 0) & (i < CHUNKS))
+        def _():
+            dx_tile(i)
+
+        w = i - (DH - KBLOCKS)
+
+        @pl.when((s == 1) & (w >= 0) & (w < 2 * UNITS))
+        def _():
+            dw_tile(lax.div(w, 2), lax.rem(w, 2))
 
         for off, event in (
             (E12, e12), (E11, e11), (E10, e10), (E9, e9), (E8, e8), (E7, e7), (E6, e6),
             (E5, e5), (E4, e4), (E3, e3), (E2, e2), (E1, e1), (0, lambda k: send_d(k).start()),
         ):
             at = t - FIRST - off
-            k = 2 * lax.div(at, 4) + lax.rem(at, 4)
-
-            @pl.when((at >= 0) & (lax.rem(at, 4) < 2) & (k < CHUNKS))
+            k = lax.div(at, 2)
+
+            @pl.when((at >= 0) & (lax.rem(at, 2) == 0) & (k < CHUNKS))
             def _(event=event, k=k):
                 event(k)
 
@@ -496,7 +495,7 @@
             dma((2,)), dma((4,)), dma((4,)), dma((8,)),
             dma((8,)), dma((8,)), dma((8,)), dma((8,)), dma((4,)), dma((4,)),
             dma((8,)), dma((8,)), dma((8,)), dma((8,)), dma((8,)), dma((8,)),
-            dma((8,)), dma((8,)), dma((8,)), dma((8,)),
+            dma((16,)), dma((16,)), dma((16,)), dma((16,)),
         ],
         compiler_params=pltpu.CompilerParams(
             collective_id=0, has_side_effects=True, vmem_limit_bytes=64_000_000
@@ -506,18 +505,67 @@
     )(x, dy, gate, up, w_gate, w_up, w_down)
 
 
-def tail_kernel(hid, dy, dx_in, dw_in, dx, dw_gate, dw_up, dw_down):
+def tail_kernel(hid, dy, dx_in, dw_in, dx, dw_gate, dw_up, dw_down, dx_buf, dw_buf, in_sem, out_sem):
+    i, n = pl.program_id(0), pl.num_programs(0)
+    slots, dx_rows, _ = dx_buf.shape
+    dw_rows = dw_buf.shape[2]
+
+    def loads(j):
+        s = lax.rem(j, slots)
+        a = pl.ds(pl.multiple_of(j * dx_rows, dx_rows), dx_rows)
+        b = pl.ds(pl.multiple_of(j * dw_rows, dw_rows), dw_rows)
+        return (
+            pltpu.make_async_copy(dx_in.at[a], dx_buf.at[s], in_sem.at[s, 0]),
+            pltpu.make_async_copy(dw_in.at[0, b], dw_buf.at[s, 0], in_sem.at[s, 1]),
+            pltpu.make_async_copy(dw_in.at[1, b], dw_buf.at[s, 1], in_sem.at[s, 2]),
+        )
+
+    def stores(j):
+        s = lax.rem(j, slots)
+        a = pl.ds(pl.multiple_of(j * dx_rows, dx_rows), dx_rows)
+        b = pl.ds(pl.multiple_of(j * dw_rows, dw_rows), dw_rows)
+        return (
+            pltpu.make_async_copy(dx_buf.at[s], dx.at[a], out_sem.at[s, 0]),
+            pltpu.make_async_copy(dw_buf.at[s, 0], dw_gate.at[b], out_sem.at[s, 1]),
+            pltpu.make_async_copy(dw_buf.at[s, 1], dw_up.at[b], out_sem.at[s, 2]),
+        )
+
+    ahead = slots // 2
+
+    @pl.when(i == 0)
+    def _():
+        for j in range(ahead):
+            for c in loads(j):
+                c.start()
+
+    @pl.when(i >= ahead)
+    def _():
+        for c in stores(i - ahead):
+            c.wait()
+
+    @pl.when(i + ahead < n)
+    def _():
+        for c in loads(i + ahead):
+            c.start()
+
+    for c in loads(i):
+        c.wait()
+    for c in stores(i):
+        c.start()
     dw_down[...] = dot(hid[...], dy[...], TN).astype(BF)
-    dx[...] = dx_in[...]
-    dw_gate[...] = dw_in[0]
-    dw_up[...] = dw_in[1]
+
+    @pl.when(i == n - 1)
+    def _():
+        for j in range(ahead):
+            for c in stores(n - ahead + j):
+                c.wait()
 
 
 def tail_call(hid, dy, dx, dw):
     rows, cols = dy.shape
     ff = hid.shape[1]
-    n = UNITS
-    spec = pl.BlockSpec
+    n, slots = UNITS, 4
+    spec, anywhere = pl.BlockSpec, pl.BlockSpec(memory_space=pl.ANY)
     return pl.pallas_call(
         tail_kernel,
         grid=(n,),
@@ -530,15 +578,16 @@
         in_specs=[
             spec((rows, ff), lambda i: (0, 0)),
             spec((rows, cols // n), lambda i: (0, i)),
-            spec((rows // n, cols), lambda i: (i, 0)),
-            spec((2, cols // n, ff), lambda i: (0, i, 0)),
+            anywhere,
+            anywhere,
         ],
-        out_specs=(
-            spec((rows // n, cols), lambda i: (i, 0)),
-            spec((cols // n, ff), lambda i: (i, 0)),
-            spec((cols // n, ff), lambda i: (i, 0)),
-            spec((ff, cols // n), lambda i: (0, i)),
-        ),
+        out_specs=(anywhere, anywhere, anywhere, spec((ff, cols // n), lambda i: (0, i))),
+        scratch_shapes=[
+            pltpu.VMEM((slots, rows // n, cols), BF),
+            pltpu.VMEM((slots, 2, cols // n, ff), BF),
+            pltpu.SemaphoreType.DMA((slots, 3)),
+            pltpu.SemaphoreType.DMA((slots, 3)),
+        ],
         compiler_params=pltpu.CompilerParams(vmem_limit_bytes=60_000_000),
         cost_estimate=pl.CostEstimate(
             flops=2 * rows * cols * ff, bytes_accessed=180 << 20, transcendentals=0

time: 395 us -> 340 us (0.86)
  Pallas kernels: 394 us -> 338 us
    pallas_call x1, Pallas kernels: 320 us -> 274 us  [main_call(): pl.pallas_call(main_kernel, out_shape=(jax.ShapeDtypeStruct((rows, cols),...]
    pallas_call x1, Pallas kernels: 74.1 us -> 63.5 us  [tail_call(): pl.pallas_call(tail_kernel, grid=(n,), out_shape=(jax.ShapeDtypeStruct((r...]
where the time goes in v2:
time: 340 us; the launch traced here: 338 us
  Pallas kernels  338 us (99%)
    pallas_call x1, Pallas kernels, main_call(): pl.pallas_call(main_kernel, out_shape=(jax.ShapeDtypeStruct((rows, cols),...  274 us
    pallas_call x1, Pallas kernels, tail_call(): pl.pallas_call(tail_kernel, grid=(n,), out_shape=(jax.ShapeDtypeStruct((r...  63.5 us

profile of v2, /device:TPU:0, one launch (start us, length us, event | category | flops | bytes accessed | tf_op | source)
XLA Modules:
  0.0 338.3 jit_solution(1671007992496306166)
XLA Ops:
  0.6 274.2 %dx_reduce.1 = (bf16[2048,8192]{1,0:T(8,128)(2,1)}, bf16[2048,1024]{1,0:T(8,128)(2,1)}, bf16[2,8192,1024]{2,1,0:T(8,128)(2,1)}) custom-call(bf16[2048,8192]{1,0:T(8,128)(2,1)} %x.1, bf16[2048,8192]{1,0:T(8,128)(2,1)} %dy.3, bf16[2048,1024]{1,0:T(8,128)(2,1)} %gate.1, bf16[2048,1024]{1,0:T(8,128)(2,1)} %up.1, bf16[8192,1024]{1,0:T(8,128)(2,1)} %w_gate.1, ...), custom_call_target="tpu_custom_call" | custom-call | flops 171798691840 | bytes 419430400 | tf_op jit(solution)/shard_map/dx_reduce/pallas_call | solution.py:466
  274.8 63.5 %dw_down_and_copies.1 = (bf16[2048,8192]{1,0:T(8,128)(2,1)}, bf16[8192,1024]{1,0:T(8,128)(2,1)}, bf16[8192,1024]{1,0:T(8,128)(2,1)}, bf16[1024,8192]{1,0:T(8,128)(2,1)}) custom-call(bf16[2048,1024]{1,0:T(8,128)(2,1)} %get-tuple-element.7.hid, bf16[2048,8192]{1,0:T(8,128)(2,1)} %dy.3, bf16[2048,8192]{1,0:T(8,128)(2,1)} %get-tuple-element.8.dx_in, ...), custom_call_target="tpu_custom_call" | custom-call | flops 34359738368 | bytes 188743680 | tf_op jit(solution)/shard_map/dw_down_and_copies/pallas_call | solution.py:569

commit v3 on v2

v3 whole, which is shorter than its diff:
```python
import jax
import jax.numpy as jnp
from jax import lax
from jax.experimental import pallas as pl
from jax.experimental.pallas import tpu as pltpu
from jax.sharding import PartitionSpec as P

BF, F32 = jnp.bfloat16, jnp.float32
MESH = pl.DeviceIdType.MESH
NT = (((1,), (1,)), ((), ()))
TN = (((0,), (0,)), ((), ()))

QUARTERS = 4
COLS = 8
TILES = QUARTERS * COLS
KBLOCKS = 4
UNITS = 16
DH = QUARTERS * KBLOCKS
FIRST = KBLOCKS
LEAD = 4
STEPS = dict(
    e1=(1, 15), e2=(3, 16), e3=(4, 16), e4=(6, 16), e5=(9, 16), e6=(14, 16),
    e8=(15, 16), e9=(19, 16), e10=(24, 17), e11=(35, 15), e12=(44, 16),
)
FILLERS = DH - KBLOCKS + 2 * UNITS
LAST_STEP = STEPS["e12"][0] + STEPS["e12"][1] * (TILES - 1) // 8
TICKS = FIRST + max(LEAD + 2 * FILLERS, LAST_STEP + 1)
N_TERM, N_RD, N_S1, N_R1, N_S2, N_Z, N_R3, N_SEM = 3, 4, 4, 6, 8, 8, 8, 16


def dot(a, b, dims):
    return lax.dot_general(a, b, dims, preferred_element_type=F32)


def add_rows(dst, a, b, rows, block):
    def body(i, _):
        r = pl.ds(pl.multiple_of(i * block, block), block)
        dst[r] = (a[r].astype(F32) + b[r].astype(F32)).astype(BF)

    lax.fori_loop(0, rows // block, body, None)


def main_kernel(
    x, dy, gate, up, w_gate, w_up, w_down, dx, hid, dw,
    d, w_buf, wd_buf, dy_buf, x_buf, g_buf, u_buf, acc, h_buf, o_buf,
    term, r_d, s1, r_1, s2, z_r, z_l, r_3,
    w_sem, dh_sem, x_sem, gu_sem, h_sem, o_sem, loc_sem,
    d_snd, d_rcv, s1_snd, s1_rcv, zr_snd, zr_rcv, zl_snd, zl_rcv, s3_snd, s3_rcv,
    gr_snd, gr_rcv, gl_snd, gl_rcv, a1_snd, a1_rcv, ad_snd, ad_rcv,
):
    rows, cols = dy.shape
    ff = gate.shape[1]
    qr, nc, kb, xt = rows // QUARTERS, cols // COLS, cols // KBLOCKS, cols // UNITS
    half, quart, piece = qr // 2, qr // 4, qr // 16

    me = lax.axis_index("tp")
    core, z = lax.rem(me, 2), lax.rem(lax.div(me, 2), 4)
    y, xx = lax.rem(lax.div(me, 8), 2), lax.div(me, 16)
    n_d = me + 1 - 2 * core
    n_x, n_y = me + 16 * (1 - 2 * xx), me + 8 * (1 - 2 * y)
    n_r, n_l = me + 2, me - 2

    def copy(src, dst, sem):
        return pltpu.make_async_copy(src, dst, sem)

    def remote(src, dst, snd, rcv, to):
        return pltpu.make_async_remote_copy(
            src_ref=src, dst_ref=dst, send_sem=snd, recv_sem=rcv,
            device_id={"tp": to}, device_id_type=MESH,
        )

    def dh_loads(m):
        q, j, slot = lax.div(m, KBLOCKS), lax.rem(m, KBLOCKS), lax.rem(m, 2)
        k = pl.ds(pl.multiple_of(j * kb, kb), kb)
        r = pl.ds(pl.multiple_of(q * qr, qr), qr)
        return (
            copy(dy.at[r, k], dy_buf.at[slot], dh_sem.at[0, slot]),
            copy(w_down.at[:, k], wd_buf.at[slot], dh_sem.at[1, slot]),
        )

    def gu_loads(q):
        r = pl.ds(pl.multiple_of(q * qr, qr), qr)
        return copy(gate.at[r], g_buf, gu_sem.at[0]), copy(up.at[r], u_buf, gu_sem.at[1])

    def w_loads(k):
        slot = lax.rem(k, 2)
        r = pl.ds(pl.multiple_of(lax.rem(k, COLS) * nc, nc), nc)
        return (
            copy(w_gate.at[r], w_buf.at[slot, :, pl.ds(0, ff)], w_sem.at[0, slot]),
            copy(w_up.at[r], w_buf.at[slot, :, pl.ds(ff, ff)], w_sem.at[1, slot]),
        )

    def x_load(u):
        slot = lax.rem(u, 2)
        return copy(x.at[:, pl.ds(pl.multiple_of(u * xt, xt), xt)], x_buf.at[slot], x_sem.at[slot])

    def o_store(u, j):
        return copy(o_buf.at[j], dw.at[j, pl.ds(pl.multiple_of(u * xt, xt), xt)], o_sem.at[j])

    def h_store(q):
        return copy(h_buf, hid.at[pl.ds(pl.multiple_of(q * qr, qr), qr)], h_sem)

    def go(*copies):
        for c in copies:
            c.start()

    def wait(*copies):
        for c in copies:
            c.wait()

    go(*dh_loads(0))
    go(*dh_loads(1))
    go(*gu_loads(0))
    go(*w_loads(0))
    go(*w_loads(1))

    barrier = pltpu.get_barrier_semaphore()
    for to in (n_d, n_x, n_y):
        pl.semaphore_signal(barrier, inc=1, device_id={"tp": to}, device_id_type=MESH)

    @pl.when(z > 0)
    def _():
        pl.semaphore_signal(barrier, inc=1, device_id={"tp": n_l}, device_id_type=MESH)

    @pl.when(z < 3)
    def _():
        pl.semaphore_signal(barrier, inc=1, device_id={"tp": n_r}, device_id_type=MESH)

    pl.semaphore_wait(barrier, jnp.where((z > 0) & (z < 3), 5, 4))

    first_bit, third_bit = (xx, y), (y, xx)
    first_to, third_to = (n_x, n_y), (n_y, n_x)
    hc = nc // 2

    def at_out(i, c, row, count, width=hc):
        r = lax.div(i, COLS) * qr + core * half + row
        k = lax.rem(i, COLS) * nc + c * hc
        return dx.at[pl.ds(pl.multiple_of(r, piece), count), pl.ds(pl.multiple_of(k, hc), width)]

    def slot_of(i, count):
        return lax.rem(i, count)

    def send_d(i):
        s, t = slot_of(i, N_TERM), slot_of(i, N_RD)
        src = term.at[s, pl.ds(pl.multiple_of((1 - core) * half, half), half)]
        return remote(src, r_d.at[t], d_snd.at[s], d_rcv.at[t], n_d)

    def send_1(i, c):
        s, t = slot_of(i, N_S1), slot_of(i, N_R1)
        src = s1.at[s, c, pl.ds(pl.multiple_of((1 - first_bit[c]) * quart, quart), quart)]
        return remote(src, r_1.at[t, c], s1_snd.at[s, c], s1_rcv.at[t, c], first_to[c])

    def send_z(i, c, right, row, count):
        s, t = slot_of(i, N_S2), slot_of(i, N_Z)
        src = s2.at[s, c, pl.ds(row * piece, count * piece)]
        buf, snd, rcv, to = (z_r, zr_snd, zr_rcv, n_r) if right else (z_l, zl_snd, zl_rcv, n_l)
        return remote(src, buf.at[t, c, pl.ds(0, count * piece)], snd.at[t, c], rcv.at[t, c], to)

    def own_piece(i, c):
        return s2.at[slot_of(i, N_S2), c, pl.ds(pl.multiple_of(z * piece, piece), piece)]

    def send_3(i, c):
        t = slot_of(i, N_R3)
        return remote(own_piece(i, c), r_3.at[t, c], s3_snd.at[t, c], s3_rcv.at[t, c], third_to[c])

    def keep_final(i, c):
        out = at_out(i, c, first_bit[c] * quart + z * piece, piece)
        return copy(own_piece(i, c), out, loc_sem.at[slot_of(i, N_SEM), c])

    def gather_z(i, c, right, first, count, fresh=False):
        ref = at_out(i, c, first_bit[c] * quart + first * piece, count * piece)
        snd, rcv, to = (gr_snd, gr_rcv, n_r) if right else (gl_snd, gl_rcv, n_l)
        s = slot_of(i, N_SEM)
        return remote(own_piece(i, c) if fresh else ref, ref, snd.at[s, c], rcv.at[s, c], to)

    def gather_1(i, c):
        ref, s = at_out(i, c, first_bit[c] * quart, quart), slot_of(i, N_SEM)
        return remote(ref, ref, a1_snd.at[s, c], a1_rcv.at[s, c], first_to[c])

    def gather_d(i):
        ref, s = at_out(i, 0, 0, half, nc), slot_of(i, N_SEM)
        return remote(ref, ref, ad_snd.at[s], ad_rcv.at[s], n_d)

    def on_line(*cases):
        for zz, body in cases:

            @pl.when(z == zz)
            def _(body=body):
                body()

    def both(body):
        for c in (0, 1):
            body(c)

    def add_piece(i, c, right, first, count):
        buf = z_r if right else z_l
        mine = s2.at[slot_of(i, N_S2), c, pl.ds(first * piece, count * piece)]
        add_rows(mine, mine, buf.at[slot_of(i, N_Z), c, pl.ds(0, count * piece)], count * piece, piece)

    def e12(i):
        gather_d(i).wait()
        both(lambda c: gather_1(i, c).wait_send())

        def middle(rights, lefts):
            def body():
                for c in (0, 1):
                    gather_z(i, c, True, *rights).wait_send()
                    gather_z(i, c, False, *lefts).wait_send()

            return body

        on_line((1, middle((0, 2), (1, 3))), (2, middle((0, 3), (2, 2))))

    def e11(i):
        both(lambda c: gather_1(i, c).wait_recv())
        gather_d(i).start()

    def e10(i):
        on_line(
            (3, lambda: both(lambda c: gather_z(i, c, True, 0, 3).wait_recv())),
            (0, lambda: both(lambda c: gather_z(i, c, False, 1, 3).wait_recv())),
        )
        both(lambda c: gather_1(i, c).start())

    def pass_on(i, right, got, gives):
        def body():
            for c in (0, 1):
                gather_z(i, c, right, *got).wait_recv()
                gather_z(i, c, right, *gives).start()

        return body

    def e9(i):
        on_line((2, pass_on(i, True, (0, 2), (0, 3))), (1, pass_on(i, False, (2, 2), (1, 3))))

    def e8(i):
        both(lambda c: keep_final(i, c).wait())
        on_line(
            (0, lambda: both(lambda c: gather_z(i, c, True, 0, 1, True).wait_send())),
            (1, pass_on(i, True, (0, 1), (0, 2))),
            (2, pass_on(i, False, (3, 1), (2, 2))),
            (3, lambda: both(lambda c: gather_z(i, c, False, 3, 1, True).wait_send())),
        )

    def e6(i):
        for c in (0, 1):
            send_3(i, c).wait()
            add_rows(own_piece(i, c), own_piece(i, c), r_3.at[slot_of(i, N_R3), c], piece, piece)

        def sent(rights, lefts):
            def body():
                for c in (0, 1):
                    if rights:
                        send_z(i, c, True, *rights).wait_send()
                    if lefts:
                        send_z(i, c, False, *lefts).wait_send()

            return body

        on_line(
            (0, sent((1, 3), None)),
            (1, sent((2, 2), (0, 1))),
            (2, sent((3, 1), (0, 2))),
            (3, sent(None, (0, 3))),
        )
        both(lambda c: keep_final(i, c).start())
        on_line(
            (0, lambda: both(lambda c: gather_z(i, c, True, 0, 1, True).start())),
            (3, lambda: both(lambda c: gather_z(i, c, False, 3, 1, True).start())),
        )

    def take(i, right, first, count, gives=None):
        def body():
            for c in (0, 1):
                send_z(i, c, right, first, count).wait_recv()
                add_piece(i, c, right, first, count)
                if gives:
                    send_z(i, c, right, *gives).start()

        return body

    def e5(i):
        on_line((3, take(i, True, 3, 1)), (0, take(i, False, 0, 1)))
        both(lambda c: send_3(i, c).start())

    def e4(i):
        on_line((2, take(i, True, 2, 2, (3, 1))), (1, take(i, False, 0, 2, (0, 1))))

    def e3(i):
        on_line((1, take(i, True, 1, 3, (2, 2))), (2, take(i, False, 0, 3, (0, 2))))

    def e2(i):
        for c in (0, 1):
            send_1(i, c).wait()
            kept = s1.at[slot_of(i, N_S1), c, pl.ds(pl.multiple_of(first_bit[c] * quart, quart), quart)]
            add_rows(s2.at[slot_of(i, N_S2), c], kept, r_1.at[slot_of(i, N_R1), c], quart, piece)
            on_line(
                (0, lambda c=c: send_z(i, c, True, 1, 3).start()),
                (3, lambda c=c: send_z(i, c, False, 0, 3).start()),
            )

    def e1(i):
        send_d(i).wait_recv()
        got = r_d.at[slot_of(i, N_RD)]
        for part in (0, 1):
            for c in (0, 1):
                b = first_bit[c] if part else 1 - first_bit[c]
                r = pl.ds(pl.multiple_of(b * quart, quart), quart)
                own = pl.ds(pl.multiple_of(core * half + b * quart, quart), quart)
                k = pl.ds(c * hc, hc)
                add_rows(
                    s1.at[slot_of(i, N_S1), c, r], term.at[slot_of(i, N_TERM), own, k], got.at[r, k], quart, piece
                )
        send_d(i).wait_send()
        both(lambda c: send_1(i, c).start())

    def e0(i):
        send_d(i).start()

    def activation(q):
        wait(*gu_loads(q))

        @pl.when(q > 0)
        def _():
            h_store(q - 1).wait()

        step = min(16, qr)

        def body(i, _):
            r = pl.ds(pl.multiple_of(i * step, step), step)
            to = pl.ds(pl.multiple_of(q * qr + i * step, step), step)
            g, u, dh = g_buf[r].astype(F32), u_buf[r].astype(F32), acc[r]
            sig = jax.nn.sigmoid(g)
            silu = g * sig
            h_buf[r] = (silu * u).astype(BF)
            d[to, pl.ds(ff, ff)] = (dh * silu).astype(BF)
            d[to, pl.ds(0, ff)] = (dh * u * (sig + silu * (1.0 - sig))).astype(BF)

        lax.fori_loop(0, qr // step, body, None)
        h_store(q).start()

        @pl.when(q + 1 < QUARTERS)
        def _():
            go(*gu_loads(q + 1))

    def dh_tile(m):
        q, j, slot = lax.div(m, KBLOCKS), lax.rem(m, KBLOCKS), lax.rem(m, 2)
        wait(*dh_loads(m))
        acc[...] = jnp.where(j == 0, 0.0, acc[...]) + dot(dy_buf[slot], wd_buf[slot], NT)

        @pl.when(m + 2 < DH)
        def _():
            go(*dh_loads(m + 2))

        @pl.when(j == KBLOCKS - 1)
        def _():
            activation(q)

    def dx_tile(k):
        slot = lax.rem(k, 2)
        r = pl.ds(pl.multiple_of(lax.div(k, COLS) * qr, qr), qr)
        wait(*w_loads(k))
        term[lax.rem(k, N_TERM)] = dot(d[r], w_buf[slot], NT).astype(BF)

        @pl.when(k + 2 < TILES)
        def _():
            go(*w_loads(k + 2))

    def dw_tile(u, j):
        slot = lax.rem(u, 2)

        @pl.when(j == 0)
        def _():
            x_load(u).wait()

        @pl.when(u > 0)
        def _():
            o_store(u - 1, j).wait()

        o_buf[j] = dot(x_buf[slot], d[:, pl.ds(pl.multiple_of(j * ff, ff), ff)], TN).astype(BF)
        o_store(u, j).start()

        @pl.when((j == 1) & (u + 2 < UNITS))
        def _():
            x_load(u + 2).start()

    steps = dict(e1=e1, e2=e2, e3=e3, e4=e4, e5=e5, e6=e6, e8=e8, e9=e9, e10=e10, e11=e11, e12=e12)

    def tick(t, _):
        n = t - FIRST - LEAD
        i, odd = lax.div(n, 2), lax.rem(n, 2)

        @pl.when((t < FIRST) | ((odd == 1) & (i < DH - KBLOCKS)))
        def _():
            dh_tile(jnp.where(t < FIRST, t, KBLOCKS + i))

        @pl.when(t == FIRST)
        def _():
            go(x_load(0), x_load(1))

        tile = jnp.where(n < 0, t - FIRST, LEAD + i)
        has_tile = (t >= FIRST) & ((n < 0) | (odd == 0)) & (tile < TILES)

        @pl.when(has_tile)
        def _():
            dx_tile(tile)

        w = i - (DH - KBLOCKS)

        @pl.when((odd == 1) & (w >= 0) & (w < 2 * UNITS))
        def _():
            dw_tile(lax.div(w, 2), lax.rem(w, 2))

        for name, event in reversed(steps.items()):
            base, pace = STEPS[name]
            at = t - FIRST - base
            j = lax.div(at * 8 + pace - 1, pace)

            @pl.when((at >= 0) & (j < TILES) & (lax.div(j * pace, 8) == at))
            def _(event=event, j=j):
                event(j)

        @pl.when(has_tile)
        def _():
            e0(tile)

    lax.fori_loop(0, TICKS, tick, None)
    h_store(QUARTERS - 1).wait()
    wait(o_store(UNITS - 1, 0), o_store(UNITS - 1, 1))


def main_call(x, dy, gate, up, w_gate, w_up, w_down):
    rows, cols = dy.shape
    ff = gate.shape[1]
    qr, nc, kb, xt = rows // QUARTERS, cols // COLS, cols // KBLOCKS, cols // UNITS
    half, quart, piece, hc = qr // 2, qr // 4, qr // 16, nc // 2
    dma = pltpu.SemaphoreType.DMA
    vmem = pltpu.VMEM
    anywhere = pl.BlockSpec(memory_space=pl.ANY)
    flops = 2 * rows * cols * ff * 5
    return pl.pallas_call(
        main_kernel,
        out_shape=(
            jax.ShapeDtypeStruct((rows, cols), BF),
            jax.ShapeDtypeStruct((rows, ff), BF),
            jax.ShapeDtypeStruct((2, cols, ff), BF),
        ),
        in_specs=[anywhere] * 7,
        out_specs=(anywhere,) * 3,
        scratch_shapes=[
            vmem((rows, 2 * ff), BF),
            vmem((2, nc, 2 * ff), BF),
            vmem((2, ff, kb), BF),
            vmem((2, qr, kb), BF),
            vmem((2, rows, xt), BF),
            vmem((qr, ff), BF),
            vmem((qr, ff), BF),
            vmem((qr, ff), F32),
            vmem((qr, ff), BF),
            vmem((2, xt, ff), BF),
            vmem((N_TERM, qr, nc), BF),
            vmem((N_RD, half, nc), BF),
            vmem((N_S1, 2, half, hc), BF),
            vmem((N_R1, 2, quart, hc), BF),
            vmem((N_S2, 2, quart, hc), BF),
            vmem((N_Z, 2, 3 * piece, hc), BF),
            vmem((N_Z, 2, 3 * piece, hc), BF),
            vmem((N_R3, 2, piece, hc), BF),
            dma((2, 2)), dma((2, 2)), dma((2,)), dma((2,)), dma, dma((2,)), dma((N_SEM, 2)),
            dma((N_TERM,)), dma((N_RD,)), dma((N_S1, 2)), dma((N_R1, 2)),
            dma((N_Z, 2)), dma((N_Z, 2)), dma((N_Z, 2)), dma((N_Z, 2)), dma((N_R3, 2)), dma((N_R3, 2)),
            dma((N_SEM, 2)), dma((N_SEM, 2)), dma((N_SEM, 2)), dma((N_SEM, 2)),
            dma((N_SEM, 2)), dma((N_SEM, 2)), dma((N_SEM,)), dma((N_SEM,)),
        ],
        compiler_params=pltpu.CompilerParams(
            collective_id=0, has_side_effects=True, vmem_limit_bytes=64_000_000
        ),
        cost_estimate=pl.CostEstimate(flops=flops, bytes_accessed=400 << 20, transcendentals=rows * ff),
        name="dx_reduce",
    )(x, dy, gate, up, w_gate, w_up, w_down)


def tail_kernel(hid, dy, dx_in, dw_in, dx, dw_gate, dw_up, dw_down, dx_buf, dw_buf, in_sem, out_sem):
    i, n = pl.program_id(0), pl.num_programs(0)
    slots, dx_rows, _ = dx_buf.shape
    dw_rows = dw_buf.shape[2]

    def loads(j):
        s = lax.rem(j, slots)
        a = pl.ds(pl.multiple_of(j * dx_rows, dx_rows), dx_rows)
        b = pl.ds(pl.multiple_of(j * dw_rows, dw_rows), dw_rows)
        return (
            pltpu.make_async_copy(dx_in.at[a], dx_buf.at[s], in_sem.at[s, 0]),
            pltpu.make_async_copy(dw_in.at[0, b], dw_buf.at[s, 0], in_sem.at[s, 1]),
            pltpu.make_async_copy(dw_in.at[1, b], dw_buf.at[s, 1], in_sem.at[s, 2]),
        )

    def stores(j):
        s = lax.rem(j, slots)
        a = pl.ds(pl.multiple_of(j * dx_rows, dx_rows), dx_rows)
        b = pl.ds(pl.multiple_of(j * dw_rows, dw_rows), dw_rows)
        return (
            pltpu.make_async_copy(dx_buf.at[s], dx.at[a], out_sem.at[s, 0]),
            pltpu.make_async_copy(dw_buf.at[s, 0], dw_gate.at[b], out_sem.at[s, 1]),
            pltpu.make_async_copy(dw_buf.at[s, 1], dw_up.at[b], out_sem.at[s, 2]),
        )

    ahead = slots // 2

    @pl.when(i == 0)
    def _():
        for j in range(ahead):
            for c in loads(j):
                c.start()

    @pl.when(i >= ahead)
    def _():
        for c in stores(i - ahead):
            c.wait()

    @pl.when(i + ahead < n)
    def _():
        for c in loads(i + ahead):
            c.start()

    for c in loads(i):
        c.wait()
    for c in stores(i):
        c.start()
    dw_down[...] = dot(hid[...], dy[...], TN).astype(BF)

    @pl.when(i == n - 1)
    def _():
        for j in range(ahead):
            for c in stores(n - ahead + j):
                c.wait()


def tail_call(hid, dy, dx, dw):
    rows, cols = dy.shape
    ff = hid.shape[1]
    n, slots = UNITS, 4
    spec, anywhere = pl.BlockSpec, pl.BlockSpec(memory_space=pl.ANY)
    return pl.pallas_call(
        tail_kernel,
        grid=(n,),
        out_shape=(
            jax.ShapeDtypeStruct((rows, cols), BF),
            jax.ShapeDtypeStruct((cols, ff), BF),
            jax.ShapeDtypeStruct((cols, ff), BF),
            jax.ShapeDtypeStruct((ff, cols), BF),
        ),
        in_specs=[
            spec((rows, ff), lambda i: (0, 0)),
            spec((rows, cols // n), lambda i: (0, i)),
            anywhere,
            anywhere,
        ],
        out_specs=(anywhere, anywhere, anywhere, spec((ff, cols // n), lambda i: (0, i))),
        scratch_shapes=[
            pltpu.VMEM((slots, rows // n, cols), BF),
            pltpu.VMEM((slots, 2, cols // n, ff), BF),
            pltpu.SemaphoreType.DMA((slots, 3)),
            pltpu.SemaphoreType.DMA((slots, 3)),
        ],
        compiler_params=pltpu.CompilerParams(vmem_limit_bytes=60_000_000),
        cost_estimate=pl.CostEstimate(
            flops=2 * rows * cols * ff, bytes_accessed=180 << 20, transcendentals=0
        ),
        name="dw_down_and_copies",
    )(hid, dy, dx, dw)


def solution(mesh):
    def step(x, dy, gate, up, w_gate, w_up, w_down):
        dx, hid, dw = main_call(x, dy, gate, up, w_gate, w_up, w_down)
        return tail_call(hid, dy, dx, dw)

    tokens, columns, rows = P("dp", None), P(None, "tp"), P("tp", None)
    return jax.shard_map(
        step,
        mesh=mesh,
        in_specs=(tokens, tokens, P("dp", "tp"), P("dp", "tp"), columns, columns, rows),
        out_specs=(tokens, P("dp", "tp"), P("dp", "tp"), P(("dp", "tp"), None)),
        check_vma=False,
    )
```

time: 340 us -> 338 us (level)
  no operation moved by 1% of the time
where the time goes in v3:
time: 338 us
  Pallas kernels  338 us (100%)
    pallas_call x1, Pallas kernels, main_call(): pl.pallas_call(main_kernel, out_shape=(jax.ShapeDtypeStruct((rows, cols),...  274 us
    pallas_call x1, Pallas kernels, tail_call(): pl.pallas_call(tail_kernel, grid=(n,), out_shape=(jax.ShapeDtypeStruct((r...  63.2 us

profile of v3, /device:TPU:0, one launch (start us, length us, event | category | flops | bytes accessed | tf_op | source)
XLA Modules:
  0.0 338.3 jit_solution(15918518493274869333)
XLA Ops:
  0.6 274.5 %dx_reduce.1 = (bf16[2048,8192]{1,0:T(8,128)(2,1)}, bf16[2048,1024]{1,0:T(8,128)(2,1)}, bf16[2,8192,1024]{2,1,0:T(8,128)(2,1)}) custom-call(bf16[2048,8192]{1,0:T(8,128)(2,1)} %x.1, bf16[2048,8192]{1,0:T(8,128)(2,1)} %dy.3, bf16[2048,1024]{1,0:T(8,128)(2,1)} %gate.1, bf16[2048,1024]{1,0:T(8,128)(2,1)} %up.1, bf16[8192,1024]{1,0:T(8,128)(2,1)} %w_gate.1, ...), custom_call_target="tpu_custom_call" | custom-call | flops 171798691840 | bytes 419430400 | tf_op jit(solution)/shard_map/dx_reduce/pallas_call | solution.py:441
  275.1 63.2 %dw_down_and_copies.1 = (bf16[2048,8192]{1,0:T(8,128)(2,1)}, bf16[8192,1024]{1,0:T(8,128)(2,1)}, bf16[8192,1024]{1,0:T(8,128)(2,1)}, bf16[1024,8192]{1,0:T(8,128)(2,1)}) custom-call(bf16[2048,1024]{1,0:T(8,128)(2,1)} %get-tuple-element.7.hid, bf16[2048,8192]{1,0:T(8,128)(2,1)} %dy.3, bf16[2048,8192]{1,0:T(8,128)(2,1)} %get-tuple-element.8.dx_in, ...), custom_call_target="tpu_custom_call" | custom-call | flops 34359738368 | bytes 188743680 | tf_op jit(solution)/shard_map/dw_down_and_copies/pallas_call | solution.py:544

commit v4 on v3

--- a/solution.py
+++ b/solution.py
@@ -16,16 +16,13 @@
 KBLOCKS = 4
 UNITS = 16
 DH = QUARTERS * KBLOCKS
-FIRST = KBLOCKS
 LEAD = 4
 STEPS = dict(
-    e1=(1, 15), e2=(3, 16), e3=(4, 16), e4=(6, 16), e5=(9, 16), e6=(14, 16),
-    e8=(15, 16), e9=(19, 16), e10=(24, 17), e11=(35, 15), e12=(44, 16),
+    e1=3, e2=7, e3=9, e4=11, e5=13, e6=16, e8=18, e9=22, e10=30, e11=34, e12=38,
 )
 FILLERS = DH - KBLOCKS + 2 * UNITS
-LAST_STEP = STEPS["e12"][0] + STEPS["e12"][1] * (TILES - 1) // 8
-TICKS = FIRST + max(LEAD + 2 * FILLERS, LAST_STEP + 1)
-N_TERM, N_RD, N_S1, N_R1, N_S2, N_Z, N_R3, N_SEM = 3, 4, 4, 6, 8, 8, 8, 16
+TRIPS = max(LEAD + FILLERS, TILES + STEPS["e12"] // 2 + 1)
+N_TERM, N_RD, N_S1, N_R1, N_S2, N_Z, N_R3, N_SEM = 2, 4, 4, 8, 8, 8, 8, 16
 
 
 def dot(a, b, dims):
@@ -386,45 +383,47 @@
 
     steps = dict(e1=e1, e2=e2, e3=e3, e4=e4, e5=e5, e6=e6, e8=e8, e9=e9, e10=e10, e11=e11, e12=e12)
 
-    def tick(t, _):
-        n = t - FIRST - LEAD
-        i, odd = lax.div(n, 2), lax.rem(n, 2)
-
-        @pl.when((t < FIRST) | ((odd == 1) & (i < DH - KBLOCKS)))
-        def _():
-            dh_tile(jnp.where(t < FIRST, t, KBLOCKS + i))
-
-        @pl.when(t == FIRST)
+    def run_steps(n, half_trip):
+        for name, event in reversed(steps.items()):
+            lag, at_half = STEPS[name] // 2, STEPS[name] % 2
+            if at_half == half_trip:
+                i = n - lag
+
+                @pl.when((i >= 0) & (i < TILES))
+                def _(event=event, i=i):
+                    event(i)
+
+    def trip(t, _):
+        n = t - KBLOCKS
+        filler = n - LEAD
+
+        @pl.when((n >= 0) & (n < TILES))
+        def _():
+            dx_tile(n)
+
+        run_steps(n, 0)
+
+        @pl.when((n >= 0) & (n < TILES))
+        def _():
+            e0(n)
+
+        @pl.when((n < 0) | ((filler >= 0) & (filler < DH - KBLOCKS)))
+        def _():
+            dh_tile(jnp.where(n < 0, n + KBLOCKS, filler + KBLOCKS))
+
+        @pl.when(n == 0)
         def _():
             go(x_load(0), x_load(1))
 
-        tile = jnp.where(n < 0, t - FIRST, LEAD + i)
-        has_tile = (t >= FIRST) & ((n < 0) | (odd == 0)) & (tile < TILES)
-
-        @pl.when(has_tile)
-        def _():
-            dx_tile(tile)
-
-        w = i - (DH - KBLOCKS)
-
-        @pl.when((odd == 1) & (w >= 0) & (w < 2 * UNITS))
+        w = filler - (DH - KBLOCKS)
+
+        @pl.when((w >= 0) & (w < 2 * UNITS))
         def _():
             dw_tile(lax.div(w, 2), lax.rem(w, 2))
 
-        for name, event in reversed(steps.items()):
-            base, pace = STEPS[name]
-            at = t - FIRST - base
-            j = lax.div(at * 8 + pace - 1, pace)
-
-            @pl.when((at >= 0) & (j < TILES) & (lax.div(j * pace, 8) == at))
-            def _(event=event, j=j):
-                event(j)
-
-        @pl.when(has_tile)
-        def _():
-            e0(tile)
-
-    lax.fori_loop(0, TICKS, tick, None)
+        run_steps(n, 1)
+
+    lax.fori_loop(0, KBLOCKS + TRIPS, trip, None)
     h_store(QUARTERS - 1).wait()
     wait(o_store(UNITS - 1, 0), o_store(UNITS - 1, 1))
 

time: 338 us -> 328 us (0.970)
  Pallas kernels: 338 us -> 327 us
    pallas_call x1, Pallas kernels: 274 us -> 264 us  [main_call(): pl.pallas_call(main_kernel, out_shape=(jax.ShapeDtypeStruct((rows, cols),...]
where the time goes in v4:
time: 328 us
  Pallas kernels  327 us (100%)
    pallas_call x1, Pallas kernels, main_call(): pl.pallas_call(main_kernel, out_shape=(jax.ShapeDtypeStruct((rows, cols),...  264 us
    pallas_call x1, Pallas kernels, tail_call(): pl.pallas_call(tail_kernel, grid=(n,), out_shape=(jax.ShapeDtypeStruct((r...  63.5 us

profile of v4, /device:TPU:0, one launch (start us, length us, event | category | flops | bytes accessed | tf_op | source)
XLA Modules:
  0.0 327.7 jit_solution(10261206777738979921)
XLA Ops:
  0.6 263.6 %dx_reduce.1 = (bf16[2048,8192]{1,0:T(8,128)(2,1)}, bf16[2048,1024]{1,0:T(8,128)(2,1)}, bf16[2,8192,1024]{2,1,0:T(8,128)(2,1)}) custom-call(bf16[2048,8192]{1,0:T(8,128)(2,1)} %x.1, bf16[2048,8192]{1,0:T(8,128)(2,1)} %dy.3, bf16[2048,1024]{1,0:T(8,128)(2,1)} %gate.1, bf16[2048,1024]{1,0:T(8,128)(2,1)} %up.1, bf16[8192,1024]{1,0:T(8,128)(2,1)} %w_gate.1, ...), custom_call_target="tpu_custom_call" | custom-call | flops 171798691840 | bytes 419430400 | tf_op jit(solution)/shard_map/dx_reduce/pallas_call | solution.py:440
  264.2 63.5 %dw_down_and_copies.1 = (bf16[2048,8192]{1,0:T(8,128)(2,1)}, bf16[8192,1024]{1,0:T(8,128)(2,1)}, bf16[8192,1024]{1,0:T(8,128)(2,1)}, bf16[1024,8192]{1,0:T(8,128)(2,1)}) custom-call(bf16[2048,1024]{1,0:T(8,128)(2,1)} %get-tuple-element.7.hid, bf16[2048,8192]{1,0:T(8,128)(2,1)} %dy.3, bf16[2048,8192]{1,0:T(8,128)(2,1)} %get-tuple-element.8.dx_in, ...), custom_call_target="tpu_custom_call" | custom-call | flops 34359738368 | bytes 188743680 | tf_op jit(solution)/shard_map/dw_down_and_copies/pallas_call | solution.py:543

commit v5 on v4

--- a/solution.py
+++ b/solution.py
@@ -108,8 +108,6 @@
     go(*dh_loads(0))
     go(*dh_loads(1))
     go(*gu_loads(0))
-    go(*w_loads(0))
-    go(*w_loads(1))
 
     barrier = pltpu.get_barrier_semaphore()
     for to in (n_d, n_x, n_y):
@@ -348,6 +346,10 @@
         @pl.when(m + 2 < DH)
         def _():
             go(*dh_loads(m + 2))
+
+        @pl.when((m == 1) | (m == KBLOCKS - 1))
+        def _():
+            go(*w_loads(lax.div(m, 2)))
 
         @pl.when(j == KBLOCKS - 1)
         def _():
@@ -479,7 +481,9 @@
     )(x, dy, gate, up, w_gate, w_up, w_down)
 
 
-def tail_kernel(hid, dy, dx_in, dw_in, dx, dw_gate, dw_up, dw_down, dx_buf, dw_buf, in_sem, out_sem):
+def tail_kernel(
+    hid, dy, dx_in, dw_in, dx, dw_gate, dw_up, dw_down, dx_buf, dw_buf, hid_buf, in_sem, out_sem, hid_sem
+):
     i, n = pl.program_id(0), pl.num_programs(0)
     slots, dx_rows, _ = dx_buf.shape
     dw_rows = dw_buf.shape[2]
@@ -508,6 +512,7 @@
 
     @pl.when(i == 0)
     def _():
+        pltpu.make_async_copy(hid, hid_buf, hid_sem).start()
         for j in range(ahead):
             for c in loads(j):
                 c.start()
@@ -526,7 +531,12 @@
         c.wait()
     for c in stores(i):
         c.start()
-    dw_down[...] = dot(hid[...], dy[...], TN).astype(BF)
+
+    @pl.when(i == 0)
+    def _():
+        pltpu.make_async_copy(hid, hid_buf, hid_sem).wait()
+
+    dw_down[...] = dot(hid_buf[...], dy[...], TN).astype(BF)
 
     @pl.when(i == n - 1)
     def _():
@@ -550,7 +560,7 @@
             jax.ShapeDtypeStruct((ff, cols), BF),
         ),
         in_specs=[
-            spec((rows, ff), lambda i: (0, 0)),
+            anywhere,
             spec((rows, cols // n), lambda i: (0, i)),
             anywhere,
             anywhere,
@@ -559,8 +569,10 @@
         scratch_shapes=[
             pltpu.VMEM((slots, rows // n, cols), BF),
             pltpu.VMEM((slots, 2, cols // n, ff), BF),
+            pltpu.VMEM((rows, ff), BF),
             pltpu.SemaphoreType.DMA((slots, 3)),
             pltpu.SemaphoreType.DMA((slots, 3)),
+            pltpu.SemaphoreType.DMA,
         ],
         compiler_params=pltpu.CompilerParams(vmem_limit_bytes=60_000_000),
         cost_estimate=pl.CostEstimate(

time: 328 us -> 329 us (level)
  no operation moved by 1% of the time
where the time goes in v5:
time: 329 us
  Pallas kernels  328 us (100%)
    pallas_call x1, Pallas kernels, main_call(): pl.pallas_call(main_kernel, out_shape=(jax.ShapeDtypeStruct((rows, cols),...  263 us
    pallas_call x1, Pallas kernels, tail_call(): pl.pallas_call(tail_kernel, grid=(n,), out_shape=(jax.ShapeDtypeStruct((r...  65.4 us

profile of v5, /device:TPU:0, one launch (start us, length us, event | category | flops | bytes accessed | tf_op | source)
XLA Modules:
  0.0 328.8 jit_solution(11834954504051323526)
XLA Ops:
  0.6 262.7 %dx_reduce.1 = (bf16[2048,8192]{1,0:T(8,128)(2,1)}, bf16[2048,1024]{1,0:T(8,128)(2,1)}, bf16[2,8192,1024]{2,1,0:T(8,128)(2,1)}) custom-call(bf16[2048,8192]{1,0:T(8,128)(2,1)} %x.1, bf16[2048,8192]{1,0:T(8,128)(2,1)} %dy.3, bf16[2048,1024]{1,0:T(8,128)(2,1)} %gate.1, bf16[2048,1024]{1,0:T(8,128)(2,1)} %up.1, bf16[8192,1024]{1,0:T(8,128)(2,1)} %w_gate.1, ...), custom_call_target="tpu_custom_call" | custom-call | flops 171798691840 | bytes 419430400 | tf_op jit(solution)/shard_map/dx_reduce/pallas_call | solution.py:442
  263.4 65.4 %dw_down_and_copies.1 = (bf16[2048,8192]{1,0:T(8,128)(2,1)}, bf16[8192,1024]{1,0:T(8,128)(2,1)}, bf16[8192,1024]{1,0:T(8,128)(2,1)}, bf16[1024,8192]{1,0:T(8,128)(2,1)}) custom-call(bf16[2048,1024]{1,0:T(8,128)(2,1)} %get-tuple-element.7.hid, bf16[2048,8192]{1,0:T(8,128)(2,1)} %dy.3, bf16[2048,8192]{1,0:T(8,128)(2,1)} %get-tuple-element.8.dx_in, ...), custom_call_target="tpu_custom_call" | custom-call | flops 34359738368 | bytes 188743680 | tf_op jit(solution)/shard_map/dw_down_and_copies/pallas_call | solution.py:553
